TPU v7x, 32 devices: a whole 2x2x4 slice. The times are simulated.
32 devices in a mesh: ep: 4 (over y, x), fsdp: 8 (over z, core).
Axes of the slice: x: 2, y: 2, z: 4, core: 2. Of those that a mesh axis runs over, the one named last changes fastest.
Arguments:
- train_gate: float32 [64, 2048, 1408], P('ep', 'fsdp'), may hold values from -0.1875 to 0.1875
- other_gate: bfloat16 [64, 2048, 1408], P('ep', 'fsdp'), may hold values from -0.0625 to 0.0625
- train_up: float32 [64, 2048, 1408], P('ep', 'fsdp'), may hold values from -0.1875 to 0.1875
- other_up: bfloat16 [64, 2048, 1408], P('ep', 'fsdp'), may hold values from -0.0625 to 0.0625
- router_weight: float32 [2048, 64], P('fsdp', 'ep'), may hold values from -0.125 to 0.125
- router_gain: float32 [2048], P('fsdp'), may hold values from 0.25 to 1.75
Outputs:
- ready_gate: bfloat16 [64, 2048, 1408], P('ep', None, 'fsdp')
- ready_up: bfloat16 [64, 2048, 1408], P('ep', None, 'fsdp')
- scale_gate: float32 [64, 1408], P('ep', 'fsdp')
- scale_up: float32 [64, 1408], P('ep', 'fsdp')
- serve_router: bfloat16 [2048, 64], replicated
All inputs are finite; a program needn't handle non-finite values. Where the computation divides by a largest or mean magnitude, that divisor is 1e-20 or more.
Results may differ from a plain program's by a relative error of at most 0.001.
Values may be sent and summed in bfloat16 or wider, within the bound.
A program may use at most 192 MiB of HBM per device.

v0:
```python
import functools

import jax
import jax.numpy as jnp
from jax import lax
from jax.experimental import pallas as pl
from jax.experimental.pallas import tpu as pltpu
from jax.sharding import PartitionSpec as P

LANES = 128
DEPTH = 3


def regroup(n, teams, tg, og, tu, ou, part, rg, ru, scales, router, mx, mo, nx, no, turned, blocks, own, pair, both, chips, final,
            mx_sem, mo_sem, nx_sem, no_sem, send_sem, keep_sem, recv_sem, p_send, p_recv, z_send, z_recv, f_send, f_recv, s_sem,
            row, whole, a_send, a_recv, a_keep, b_send, b_recv, b_keep):
    me, team = lax.axis_index("fsdp"), lax.axis_index("ep")
    core = lax.rem(me, 2)
    partner = me + 1 - 2 * core
    experts, rows, columns = tg.shape
    width = columns // n
    trains, others, outs = (tg, tu), (og, ou), (rg, ru)

    def loads(x, o, x_sem, o_sem, e):
        slot = lax.rem(e, 2)
        copies = []
        for t in range(2):
            copies.append(pltpu.make_async_copy(trains[t].at[e], x.at[slot, t], x_sem.at[slot, t]))
            copies.append(pltpu.make_async_copy(others[t].at[e], o.at[slot, t], o_sem.at[slot, t]))
        return copies

    def remote(src, dst, send, recv, device):
        return pltpu.make_async_remote_copy(
            src_ref=src, dst_ref=dst, send_sem=send, recv_sem=recv, device_id={"fsdp": device},
            device_id_type=pl.DeviceIdType.MESH,
        )

    def wait_bytes(ref, sem):
        pltpu.make_async_copy(ref, ref, sem).wait()

    for copy in loads(mx, mo, mx_sem, mo_sem, 0):
        copy.start()
    for copy in loads(nx, no, nx_sem, no_sem, 0):
        copy.start()

    barrier = pltpu.get_barrier_semaphore()
    for k in range(1, n):
        pl.semaphore_signal(barrier, inc=1, device_id={"fsdp": lax.rem(me + k, n)}, device_id_type=pl.DeviceIdType.MESH)
    for k in range(1, teams):
        pl.semaphore_signal(barrier, inc=1, device_id={"ep": lax.rem(team + k, teams)}, device_id_type=pl.DeviceIdType.MESH)
    pl.semaphore_wait(barrier, n + teams - 2)

    def measure(e):
        slot = lax.rem(e, 2)

        @pl.when(e + 1 < experts)
        def _():
            for copy in loads(mx, mo, mx_sem, mo_sem, e + 1):
                copy.start()

        for copy in loads(mx, mo, mx_sem, mo_sem, e):
            copy.wait()
        for t in range(2):
            for j in range(0, columns, LANES):
                latest = mx[slot, t, :, j : j + LANES] + mo[slot, t, :, j : j + LANES].astype(jnp.float32)
                own[e, t, :, j : j + LANES] = jnp.max(jnp.abs(latest), axis=0, keepdims=True)
        remote(own.at[e, 1 - core], pair.at[e], p_send.at[e], p_recv.at[e], partner).start()

    def chip_max(e):
        remote(own.at[e, 1 - core], pair.at[e], p_send.at[e], p_recv.at[e], partner).wait()
        both[e] = jnp.maximum(own[e, core], pair[e])
        for k in range(1, n // 2):
            remote(both.at[e], chips.at[e, k - 1], z_send.at[e], z_recv.at[e], lax.rem(me + 2 * k, n)).start()

    def all_max(e):
        wait_bytes(chips.at[e], z_send.at[e])
        wait_bytes(chips.at[e], z_recv.at[e])
        top = both[e]
        for k in range(1, n // 2):
            top = jnp.maximum(top, chips[e, k - 1])
        final[e, core] = top
        remote(final.at[e, core], final.at[e, core], f_send.at[e], f_recv.at[e], partner).start()

    def send(e):
        slot = lax.rem(e, 2)

        @pl.when(e + 1 < experts)
        def _():
            for copy in loads(nx, no, nx_sem, no_sem, e + 1):
                copy.start()

        for copy in loads(nx, no, nx_sem, no_sem, e):
            copy.wait()
        remote(final.at[e, core], final.at[e, core], f_send.at[e], f_recv.at[e], partner).wait()
        for t in range(2):
            for j in range(0, columns, LANES):
                latest = nx[slot, t, :, j : j + LANES] + no[slot, t, :, j : j + LANES].astype(jnp.float32)
                turned[j : j + LANES, :] = (latest / final[e, t, :, j : j + LANES]).T

            @pl.when(e >= 2)
            def _():
                wait_bytes(blocks.at[slot, t, pl.ds(0, n - 1)], send_sem.at[slot, t])
                wait_bytes(blocks.at[slot, t, 0], keep_sem.at[slot, t])

            for d in range(n):
                blocks[slot, t, d] = turned[d * width : (d + 1) * width, :].astype(jnp.bfloat16)
            place = outs[t].at[e, :, pl.ds(pl.multiple_of(me * rows, rows), rows)]
            for k in range(n):
                device = lax.rem(me + n // 2 + k, n)
                block = blocks.at[slot, t, device]
                if k == n // 2:
                    pltpu.make_async_copy(block, place, keep_sem.at[slot, t]).start()
                else:
                    remote(block, place, send_sem.at[slot, t], recv_sem.at[t, e], device).start()

    def router_rows():
        pltpu.make_async_copy(part, row.at[me], a_keep).start()
        for k in range(1, n):
            remote(part, row.at[me], a_send, a_recv, lax.rem(me + k, n)).start()

    def router_columns():
        pltpu.make_async_copy(part, row.at[me], a_keep).wait()
        wait_bytes(row.at[pl.ds(0, n - 1)], a_send)
        wait_bytes(row.at[pl.ds(0, n - 1)], a_recv)
        pltpu.make_async_copy(row, whole.at[team], b_keep).start()
        for k in range(1, teams):
            pltpu.make_async_remote_copy(
                src_ref=row, dst_ref=whole.at[team], send_sem=b_send, recv_sem=b_recv,
                device_id={"ep": lax.rem(team + k, teams)}, device_id_type=pl.DeviceIdType.MESH,
            ).start()

    def step(i, carry):
        pl.when(i >= DEPTH)(lambda: send(i - DEPTH))
        pl.when(i < experts)(lambda: measure(i))
        pl.when((i >= 1) & (i < experts + 1))(lambda: chip_max(i - 1))
        pl.when((i >= 2) & (i < experts + 2))(lambda: all_max(i - 2))
        pl.when(i == DEPTH)(router_rows)
        pl.when(i == experts)(router_columns)
        return carry

    lax.fori_loop(0, experts + DEPTH, step, 0)
    keep = pltpu.make_async_copy(final, scales, s_sem)
    keep.start()
    pltpu.make_async_copy(row, whole.at[team], b_keep).wait()
    wait_bytes(whole.at[pl.ds(0, teams - 1)], b_send)
    wait_bytes(whole.at[pl.ds(0, teams - 1)], b_recv)
    keep_router = pltpu.make_async_copy(whole, router, a_keep)
    keep_router.start()
    for slot in range(2):
        for t in range(2):
            wait_bytes(blocks.at[slot, t, pl.ds(0, n - 1)], send_sem.at[slot, t])
            wait_bytes(blocks.at[slot, t, 0], keep_sem.at[slot, t])

    def arrive(e, carry):
        for t in range(2):
            wait_bytes(outs[t].at[e, :, pl.ds(0, (n - 1) * rows)], recv_sem.at[t, e])
        return carry

    lax.fori_loop(0, experts, arrive, 0)
    keep.wait()
    keep_router.wait()


def per_device(n, teams, train_gate, other_gate, train_up, other_up, router_weight, router_gain):
    experts, rows, columns = train_gate.shape
    width = columns // n
    f32, bf16, dma = jnp.float32, jnp.bfloat16, pltpu.SemaphoreType.DMA
    ready = jax.ShapeDtypeStruct((experts, width, rows * n), bf16)
    any_space = pl.BlockSpec(memory_space=pl.ANY)
    part_router = (router_weight * router_gain[:, None]).astype(bf16).T
    ready_gate, ready_up, scales, router = pl.pallas_call(
        functools.partial(regroup, n, teams),
        out_shape=(ready, ready, jax.ShapeDtypeStruct((experts, 2, 1, columns), f32),
                   jax.ShapeDtypeStruct((teams, n) + part_router.shape, bf16)),
        in_specs=[any_space] * 4 + [pl.BlockSpec(memory_space=pltpu.VMEM)],
        out_specs=(any_space,) * 4,
        scratch_shapes=[
            pltpu.VMEM((2, 2, rows, columns), f32),
            pltpu.VMEM((2, 2, rows, columns), bf16),
            pltpu.VMEM((2, 2, rows, columns), f32),
            pltpu.VMEM((2, 2, rows, columns), bf16),
            pltpu.VMEM((columns, rows), f32),
            pltpu.VMEM((2, 2, n, width, rows), bf16),
            pltpu.VMEM((experts, 2, 1, columns), f32),
            pltpu.VMEM((experts, 1, columns), f32),
            pltpu.VMEM((experts, 1, columns), f32),
            pltpu.VMEM((experts, n // 2 - 1, 1, columns), f32),
            pltpu.VMEM((experts, 2, 1, columns), f32),
            dma((2, 2)),
            dma((2, 2)),
            dma((2, 2)),
            dma((2, 2)),
            dma((2, 2)),
            dma((2, 2)),
            dma((2, experts)),
            dma((experts,)),
            dma((experts,)),
            dma((experts,)),
            dma((experts,)),
            dma((experts,)),
            dma((experts,)),
            dma,
            pltpu.VMEM((n,) + part_router.shape, bf16),
            pltpu.VMEM((teams, n) + part_router.shape, bf16),
            dma,
            dma,
            dma,
            dma,
            dma,
            dma,
        ],
        compiler_params=pltpu.CompilerParams(collective_id=0, has_side_effects=True, vmem_limit_bytes=48 * 2**20),
        name="regroup",
    )(train_gate, other_gate, train_up, other_up, part_router)
    ready_gate, ready_up = jnp.swapaxes(ready_gate, 1, 2), jnp.swapaxes(ready_up, 1, 2)
    mine = lax.dynamic_slice_in_dim(scales, lax.axis_index("fsdp") * width, width, axis=3)
    serve_router = router.transpose(1, 3, 0, 2).reshape(n * router.shape[3], -1)
    return (ready_gate, ready_up, mine[:, 0, 0], mine[:, 1, 0], serve_router)


def solution(mesh):
    in_specs = (
        P("ep", "fsdp", None),
        P("ep", "fsdp", None),
        P("ep", "fsdp", None),
        P("ep", "fsdp", None),
        P("fsdp", "ep"),
        P("fsdp"),
    )
    out_specs = (
        P("ep", None, "fsdp"),
        P("ep", None, "fsdp"),
        P("ep", "fsdp"),
        P("ep", "fsdp"),
        P(),
    )
    return jax.shard_map(
        functools.partial(per_device, mesh.shape["fsdp"], mesh.shape["ep"]), mesh=mesh, in_specs=in_specs, out_specs=out_specs,
        check_vma=False,
    )
```

profile of v0, /device:TPU:0, one launch (start us, length us, event | category | flops | bytes accessed | tf_op | source)
XLA Modules:
  0.0 537.9 jit_solution(8379357152673201010)
XLA Ops:
  0.6 0.7 fusion.part
  1.4 518.8 %regroup.1 = (bf16[16,176,2048]{2,1,0:T(8,128)(2,1)}, bf16[16,176,2048]{2,1,0:T(8,128)(2,1)}, f32[16,2,1,1408]{3,2,1,0:T(1,128)S(1)}, bf16[4,8,16,256]{3,2,1,0:T(8,128)(2,1)S(1)}) custom-call(f32[16,256,1408]{2,1,0:T(8,128)} %tg.1, bf16[16,256,1408]{2,1,0:T(8,128)(2,1)} %og.1, f32[16,256,1408]{2,1,0:T(8,128)} %tu.1, bf16[16,256,1408]{2,1,0:T(8,128)(2,1)} %ou.1, ...), custom_call_target="tpu_custom_call" | custom-call | tf_op jit(solution)/shard_map/regroup/pallas_call | solution.py:171
  520.2 0.1 constant_dynamic-slice_fusion.1
  520.3 0.6 copy_bitcast_fusion
  520.9 0.1 copy.11
  521.0 0.0 slice-start
  521.0 0.8 copy.14
  521.8 0.0 slice-start.1
  521.8 0.0 slice-start.2
  521.8 11.6 %copy.19 = bf16[16,2048,176]{1,2,0:T(8,128)(2,1)} copy(bf16[16,2048,176]{1,2,0:T(8,128)(2,1)} %bitcast.18) | data formatting | bytes 23068672
  533.4 0.0 slice-done
  533.4 0.0 slice-done.1
  533.4 0.0 slice-done.2
  533.4 4.4 copy.20
  (1 shorter events, 0.0 us)
Async XLA Ops:
  521.0 12.4 %slice-start = ((s8[11534336]{0:T(1024)(128)(4,1)}), s8[4194304]{0:T(1024)(128)(4,1)S(1)}, s32[]{:S(2)}) async-start(s8[11534336]{0:T(1024)(128)(4,1)} %bitcast.15), calls=%async_computation | async-start | bytes 8388608
  521.8 11.6 %slice-start.1 = ((s8[11534336]{0:T(1024)(128)(4,1)}), s8[4194304]{0:T(1024)(128)(4,1)S(1)}, s32[]{:S(2)}) async-start(s8[11534336]{0:T(1024)(128)(4,1)} %bitcast.15), calls=%async_computation.1 | async-start | bytes 8388608
  521.8 11.6 %slice-start.2 = ((s8[11534336]{0:T(1024)(128)(4,1)}), s8[3145728]{0:T(1024)(128)(4,1)S(1)}, s32[]{:S(2)}) async-start(s8[11534336]{0:T(1024)(128)(4,1)} %bitcast.15), calls=%async_computation.2 | async-start | bytes 6291456
where the time goes:
time: 538 us
  Pallas kernels  519 us (96%)
  local copies, waits for them, and re-layouts  17.7 us (3%)
    pallas_call x1, Pallas kernels, per_device(): pl.pallas_call(functools.partial(regroup, n, teams), out_shape=(ready, re...  519 us
    unnamed x10, local copies, waits for them, and re-layouts  17.4 us

commit v1 on v0

--- a/solution.py
+++ b/solution.py
@@ -9,11 +9,12 @@
 
 LANES = 128
 DEPTH = 3
-
-
-def regroup(n, teams, tg, og, tu, ou, part, rg, ru, scales, router, mx, mo, nx, no, turned, blocks, own, pair, both, chips, final,
-            mx_sem, mo_sem, nx_sem, no_sem, send_sem, keep_sem, recv_sem, p_send, p_recv, z_send, z_recv, f_send, f_recv, s_sem,
-            row, whole, a_send, a_recv, a_keep, b_send, b_recv, b_keep):
+PIECES = 8
+
+
+def regroup(n, teams, tg, og, tu, ou, weight, gain, rg, ru, sg, su, router, mx, mo, nx, no, turned, blocks, own, pair, both, chips, final,
+            mx_sem, mo_sem, nx_sem, no_sem, send_sem, keep_sem, recv_sem, p_send, p_recv, z_send, z_recv, f_send, f_recv,
+            tops, part, row, whole, a_send, a_recv, a_keep, b_send, b_recv, b_keep):
     me, team = lax.axis_index("fsdp"), lax.axis_index("ep")
     core = lax.rem(me, 2)
     partner = me + 1 - 2 * core
@@ -42,6 +43,7 @@
         copy.start()
     for copy in loads(nx, no, nx_sem, no_sem, 0):
         copy.start()
+    part[...] = (weight[...] * gain[...]).astype(jnp.bfloat16)
 
     barrier = pltpu.get_barrier_semaphore()
     for k in range(1, n):
@@ -93,6 +95,7 @@
             copy.wait()
         remote(final.at[e, core], final.at[e, core], f_send.at[e], f_recv.at[e], partner).wait()
         for t in range(2):
+            tops[t, pl.ds(e, 1), :] = final[e, t]
             for j in range(0, columns, LANES):
                 latest = nx[slot, t, :, j : j + LANES] + no[slot, t, :, j : j + LANES].astype(jnp.float32)
                 turned[j : j + LANES, :] = (latest / final[e, t, :, j : j + LANES]).T
@@ -139,13 +142,20 @@
         return carry
 
     lax.fori_loop(0, experts + DEPTH, step, 0)
-    keep = pltpu.make_async_copy(final, scales, s_sem)
-    keep.start()
+    for t, out in enumerate((sg, su)):
+        for d in range(n):
+
+            @pl.when(me == d)
+            def _():
+                out[...] = tops[t, :, d * width : (d + 1) * width]
+
     pltpu.make_async_copy(row, whole.at[team], b_keep).wait()
     wait_bytes(whole.at[pl.ds(0, teams - 1)], b_send)
     wait_bytes(whole.at[pl.ds(0, teams - 1)], b_recv)
-    keep_router = pltpu.make_async_copy(whole, router, a_keep)
-    keep_router.start()
+    wide, deep = part.shape
+    for a in range(teams):
+        for d in range(n):
+            router[a * wide : (a + 1) * wide, d * deep : (d + 1) * deep] = whole[a, d]
     for slot in range(2):
         for t in range(2):
             wait_bytes(blocks.at[slot, t, pl.ds(0, n - 1)], send_sem.at[slot, t])
@@ -157,8 +167,22 @@
         return carry
 
     lax.fori_loop(0, experts, arrive, 0)
-    keep.wait()
-    keep_router.wait()
+
+
+def settle(*refs):
+    count = len(refs) // 2
+    copies = []
+    for src, dst in zip(refs[:count], refs[count:-1]):
+        rows = src.shape[0]
+        piece = max(rows // PIECES, 1) if len(src.shape) == 3 else rows
+        for i in range(0, rows, piece):
+            size = min(piece, rows - i)
+            copies.append((src.at[pl.ds(i, size)], dst.at[pl.ds(i, size)]))
+    copies = [pltpu.make_async_copy(src, dst, refs[-1].at[i]) for i, (src, dst) in enumerate(copies)]
+    for copy in copies:
+        copy.start()
+    for copy in copies:
+        copy.wait()
 
 
 def per_device(n, teams, train_gate, other_gate, train_up, other_up, router_weight, router_gain):
@@ -167,13 +191,15 @@
     f32, bf16, dma = jnp.float32, jnp.bfloat16, pltpu.SemaphoreType.DMA
     ready = jax.ShapeDtypeStruct((experts, width, rows * n), bf16)
     any_space = pl.BlockSpec(memory_space=pl.ANY)
-    part_router = (router_weight * router_gain[:, None]).astype(bf16).T
-    ready_gate, ready_up, scales, router = pl.pallas_call(
+    part = router_weight.shape[::-1]
+    scale = jax.ShapeDtypeStruct((experts, width), f32)
+    out_shape = (ready, ready, scale, scale, jax.ShapeDtypeStruct((teams * part[0], n * part[1]), bf16))
+    vmem = pl.BlockSpec(memory_space=pltpu.VMEM)
+    outs = pl.pallas_call(
         functools.partial(regroup, n, teams),
-        out_shape=(ready, ready, jax.ShapeDtypeStruct((experts, 2, 1, columns), f32),
-                   jax.ShapeDtypeStruct((teams, n) + part_router.shape, bf16)),
-        in_specs=[any_space] * 4 + [pl.BlockSpec(memory_space=pltpu.VMEM)],
-        out_specs=(any_space,) * 4,
+        out_shape=out_shape,
+        in_specs=[any_space] * 4 + [vmem] * 2,
+        out_specs=(any_space, any_space, vmem, vmem, vmem),
         scratch_shapes=[
             pltpu.VMEM((2, 2, rows, columns), f32),
             pltpu.VMEM((2, 2, rows, columns), bf16),
@@ -199,9 +225,10 @@
             dma((experts,)),
             dma((experts,)),
             dma((experts,)),
-            dma,
-            pltpu.VMEM((n,) + part_router.shape, bf16),
-            pltpu.VMEM((teams, n) + part_router.shape, bf16),
+            pltpu.VMEM((2, experts, columns), f32),
+            pltpu.VMEM(part, bf16),
+            pltpu.VMEM((n,) + part, bf16),
+            pltpu.VMEM((teams, n) + part, bf16),
             dma,
             dma,
             dma,
@@ -209,13 +236,19 @@
             dma,
             dma,
         ],
-        compiler_params=pltpu.CompilerParams(collective_id=0, has_side_effects=True, vmem_limit_bytes=48 * 2**20),
+        compiler_params=pltpu.CompilerParams(collective_id=0, has_side_effects=True, vmem_limit_bytes=28 * 2**20),
         name="regroup",
-    )(train_gate, other_gate, train_up, other_up, part_router)
-    ready_gate, ready_up = jnp.swapaxes(ready_gate, 1, 2), jnp.swapaxes(ready_up, 1, 2)
-    mine = lax.dynamic_slice_in_dim(scales, lax.axis_index("fsdp") * width, width, axis=3)
-    serve_router = router.transpose(1, 3, 0, 2).reshape(n * router.shape[3], -1)
-    return (ready_gate, ready_up, mine[:, 0, 0], mine[:, 1, 0], serve_router)
+    )(train_gate, other_gate, train_up, other_up, router_weight.T, router_gain[None])
+    ready_gate, ready_up, scale_gate, scale_up, router = pl.pallas_call(
+        settle,
+        out_shape=out_shape,
+        in_specs=[any_space] * 5,
+        out_specs=(any_space,) * 5,
+        scratch_shapes=[dma((2 * experts + 3,))],
+        compiler_params=pltpu.CompilerParams(vmem_limit_bytes=2**20),
+        name="settle",
+    )(*outs)
+    return jnp.swapaxes(ready_gate, 1, 2), jnp.swapaxes(ready_up, 1, 2), scale_gate, scale_up, router.T
 
 
 def solution(mesh):

time: 538 us -> 529 us (0.983)
  local copies, waits for them, and re-layouts: 17.7 us -> 1.39 us
  Pallas kernels: 519 us -> 527 us
    unnamed x10 -> x4, local copies, waits for them, and re-layouts: 17.4 us -> 1.39 us
    pallas_call x1 -> x2, Pallas kernels: 519 us -> 527 us  [the longest x1 519 us: per_device(): pl.pallas_call(functools.partial(regroup, n, teams), out_shape=out_shape,...]
where the time goes in v1:
time: 529 us
  Pallas kernels  527 us (100%)
    pallas_call x1, Pallas kernels, per_device(): pl.pallas_call(functools.partial(regroup, n, teams), out_shape=out_shape,...  519 us

profile of v1, /device:TPU:0, one launch (start us, length us, event | category | flops | bytes accessed | tf_op | source)
XLA Modules:
  0.0 529.0 jit_solution(447596055829420875)
XLA Ops:
  0.6 0.0 copy-start
  0.6 0.7 copy-done
  1.4 0.0 copy-start.1
  1.4 0.7 copy-done.1
  2.0 518.8 %regroup.1 = (bf16[16,176,2048]{2,1,0:T(8,128)(2,1)S(1)}, bf16[16,176,2048]{2,1,0:T(8,128)(2,1)S(1)}, f32[16,176]{1,0:T(8,128)S(1)}, f32[16,176]{1,0:T(8,128)S(1)}, bf16[64,2048]{1,0:T(8,128)(2,1)S(1)}) custom-call(f32[16,256,1408]{2,1,0:T(8,128)} %tg.1, bf16[16,256,1408]{2,1,0:T(8,128)(2,1)} %og.1, f32[16,256,1408]{2,1,0:T(8,128)} %tu.1, ...), custom_call_target="tpu_custom_call" | custom-call | tf_op jit(solution)/shard_map/regroup/pallas_call | solution.py:198
  520.9 8.1 %settle.1 = (bf16[16,176,2048]{2,1,0:T(8,128)(2,1)}, bf16[16,176,2048]{2,1,0:T(8,128)(2,1)}, f32[16,176]{1,0:T(8,128)}, f32[16,176]{1,0:T(8,128)}, bf16[64,2048]{1,0:T(8,128)(2,1)}) custom-call(bf16[16,176,2048]{2,1,0:T(8,128)(2,1)S(1)} %get-tuple-element.15.refs_0_, bf16[16,176,2048]{2,1,0:T(8,128)(2,1)S(1)} %get-tuple-element.16.refs_1_, ...), custom_call_target="tpu_custom_call" | custom-call | tf_op jit(solution)/shard_map/settle/pallas_call | solution.py:242
Async XLA Ops:
  0.6 0.7 copy-start
  1.4 0.7 copy-start.1

commit v2 on v1

v2 whole, which is shorter than its diff:
```python
import functools

import jax
import jax.numpy as jnp
from jax import lax
from jax.experimental import pallas as pl
from jax.experimental.pallas import tpu as pltpu
from jax.sharding import PartitionSpec as P

LANES = 128
LAG = 1
PIECES = 8


def regroup(n, teams, tg, og, tu, ou, part, rg, ru, sg, su, router, mx, mo, nx, no, turned, blocks,
            own, pair, both, toright, toleft, fromleft, fromright, chips, zero, mine, theirs, final, tops, row, whole,
            mx_sem, mo_sem, nx_sem, no_sem, send_sem, keep_sem, recv_sem, p_send, p_recv, z_send, z_recv, r_send, r_recv,
            l_send, l_recv, f_send, f_recv, y_send, y_recv, q_send, q_recv, a_send, a_recv, c_send, c_recv, b_send, b_recv):
    me, team = lax.axis_index("fsdp"), lax.axis_index("ep")
    core, chip = lax.rem(me, 2), lax.div(me, 2)
    partner = me + 1 - 2 * core
    line, half = n // 2, n // 2
    last = line - 1
    left = me < half
    far, near = jnp.where(left, half, 0), jnp.where(left, 0, half)
    mirror = lax.rem(me + half, n)
    experts, rows, columns = tg.shape
    width, count = columns // n, columns // LANES
    skipped = columns // 2 // LANES
    shift = jnp.where(left, skipped, 0)
    trains, others, outs = (tg, tu), (og, ou), (rg, ru)
    ahead = [1 + (last - h) * LAG for h in range(line)]
    early = (ahead[0] + 1) // 2

    def measure_loads(e, t):
        slot = lax.rem(e, 2)
        return (
            pltpu.make_async_copy(trains[t].at[e], mx.at[slot, t], mx_sem.at[slot, t]),
            pltpu.make_async_copy(others[t].at[e], mo.at[slot, t], mo_sem.at[slot, t]),
        )

    def send_loads(e, t):
        return (
            pltpu.make_async_copy(trains[t].at[e], nx.at[t], nx_sem.at[t]),
            pltpu.make_async_copy(others[t].at[e], no.at[t], no_sem.at[t]),
        )

    def remote(src, dst, send, recv, device, axis="fsdp"):
        return pltpu.make_async_remote_copy(
            src_ref=src, dst_ref=dst, send_sem=send, recv_sem=recv, device_id={axis: device},
            device_id_type=pl.DeviceIdType.MESH,
        )

    def wait_bytes(ref, sem):
        pltpu.make_async_copy(ref, ref, sem).wait()

    def largest(e, t):
        slot = lax.rem(e, 2)
        for copy in measure_loads(e, t):
            copy.wait()
        for j in range(0, columns, LANES):
            latest = mx[slot, t, :, j : j + LANES] + mo[slot, t, :, j : j + LANES].astype(jnp.float32)
            own[e, t, :, j : j + LANES] = jnp.max(jnp.abs(latest), axis=0, keepdims=True)

    def measure(e):
        @pl.when(e + 1 < experts)
        def _():
            for t in range(2):
                for copy in measure_loads(e + 1, t):
                    copy.start()

        for t in range(2):
            largest(e, t)
        remote(own.at[e, 1 - core], pair.at[e], p_send.at[e], p_recv.at[e], partner).start()

    def chip_max(e):
        remote(own.at[e, 1 - core], pair.at[e], p_send.at[e], p_recv.at[e], partner).wait()
        both[e] = jnp.maximum(own[e, core], pair[e])

    def spread(e):
        for k in range(1, line):
            remote(both.at[e], chips.at[e, k - 1], z_send.at[e], z_recv.at[e], lax.rem(me + 2 * k, n)).start()

    def hop(h, e):
        @pl.when(chip == h)
        def _():
            if h:
                wait_bytes(fromleft.at[e], r_recv.at[e])
                toright[e] = jnp.maximum(both[e], fromleft[e])
            else:
                toright[e] = both[e]
            remote(toright.at[e], fromleft.at[e], r_send.at[e], r_recv.at[e], me + 2).start()

        @pl.when(chip == last - h)
        def _():
            if h:
                wait_bytes(fromright.at[e], l_recv.at[e])
                toleft[e] = jnp.maximum(both[e], fromright[e])
            else:
                toleft[e] = both[e]
            remote(toleft.at[e], fromright.at[e], l_send.at[e], l_recv.at[e], me - 2).start()

    def share(e):
        remote(final.at[e, core], final.at[e, core], f_send.at[e], f_recv.at[e], partner).start()

    def all_direct(e):
        wait_bytes(chips.at[e], z_send.at[e])
        wait_bytes(chips.at[e], z_recv.at[e])
        top = both[e]
        for k in range(1, line):
            top = jnp.maximum(top, chips[e, k - 1])
        final[e, core] = top
        share(e)

    def all_swept(e):
        final[e, core] = both[e]

        @pl.when(chip > 0)
        def _():
            pl.when(chip == last)(lambda: wait_bytes(fromleft.at[e], r_recv.at[e]))
            wait_bytes(toleft.at[e], l_send.at[e])
            final[e, core] = jnp.maximum(final[e, core], fromleft[e])

        @pl.when(chip < last)
        def _():
            pl.when(chip == 0)(lambda: wait_bytes(fromright.at[e], l_recv.at[e]))
            wait_bytes(toright.at[e], r_send.at[e])
            final[e, core] = jnp.maximum(final[e, core], fromright[e])

        share(e)

    def stages(i, s):
        for h in range(line):
            if (ahead[h] + s) % 2:
                continue
            e = i + (ahead[h] + s) // 2
            live = (e >= early) & (e < experts)
            if h == 0:

                @pl.when(live)
                def _():
                    measure(e)
                    chip_max(e)

            if h < last:
                pl.when(live)(lambda: hop(h, e))
            else:
                pl.when(live)(lambda: all_swept(e))
                pl.when(e < early)(lambda: all_direct(e))

    def send(e, t):
        slot = lax.rem(e, 2)
        for copy in send_loads(e, t):
            copy.wait()

        @pl.when(e == 0)
        def _():
            remote(mine.at[t], theirs.at[t], q_send.at[t], q_recv.at[t], partner).wait()
            final[0, t] = jnp.maximum(mine[t], theirs[t])

        if t == 0:

            @pl.when(e > 0)
            def _():
                remote(final.at[e, core], final.at[e, core], f_send.at[e], f_recv.at[e], partner).wait()

        tops[t, pl.ds(e, 1), :] = final[e, t]
        place = outs[t].at[e, :, pl.ds(pl.multiple_of(me * rows, rows), rows)]

        def turn(p):
            j = pl.multiple_of(lax.rem(p + shift, count) * LANES, LANES)
            latest = nx[t, :, pl.ds(j, LANES)] + no[t, :, pl.ds(j, LANES)].astype(jnp.float32)
            turned[pl.ds(j, LANES), :] = (latest / final[e, t, :, pl.ds(j, LANES)]).T

        def pack(base, k):
            d = base + lax.rem(me + k, half)
            blocks[slot, t, d] = turned[pl.ds(pl.multiple_of(d * width, width), width), :].astype(jnp.bfloat16)
            if k == 0:
                pl.when(d == me)(lambda: pltpu.make_async_copy(blocks.at[slot, t, d], place, keep_sem.at[slot, t]).start())
                pl.when(d != me)(lambda: remote(blocks.at[slot, t, d], place, send_sem.at[slot, t], recv_sem.at[t, e], d).start())
            else:
                remote(blocks.at[slot, t, d], place, send_sem.at[slot, t], recv_sem.at[t, e], d).start()

        for p in range(count - skipped):
            turn(p)

        @pl.when(e >= 2)
        def _():
            wait_bytes(blocks.at[slot, t, pl.ds(0, n - 1)], send_sem.at[slot, t])
            wait_bytes(blocks.at[slot, t, 0], keep_sem.at[slot, t])

        for k in range(half):
            pack(far, k)
        for p in range(count - skipped, count):
            turn(p)
        for k in range(half):
            pack(near, k)

        @pl.when(e + 1 < experts)
        def _():
            for copy in send_loads(e + 1, t):
                copy.start()

    def router_cross():
        row[me] = part[...]
        remote(part, row.at[me], a_send, a_recv, mirror).start()

    def router_rows():
        remote(part, row.at[me], a_send, a_recv, mirror).wait()
        for k in range(1, half):
            for at in (me, mirror):
                remote(row.at[at], row.at[at], c_send, c_recv, near + lax.rem(me + k, half)).start()

    def router_columns():
        wait_bytes(row.at[pl.ds(0, 2 * (half - 1))], c_send)
        wait_bytes(row.at[pl.ds(0, 2 * (half - 1))], c_recv)
        whole[team] = row[...]
        for k in range(1, teams):
            remote(row, whole.at[team], b_send, b_recv, lax.rem(team + k, teams), "ep").start()

    def router_whole():
        wait_bytes(whole.at[pl.ds(0, teams - 1)], b_send)
        wait_bytes(whole.at[pl.ds(0, teams - 1)], b_recv)
        wide, deep = part.shape
        for a in range(teams):
            for d in range(n):
                router[a * wide : (a + 1) * wide, d * deep : (d + 1) * deep] = whole[a, d]

    for t in range(2):
        for copy in measure_loads(0, t):
            copy.start()
    barrier = pltpu.get_barrier_semaphore()
    for k in range(1, n):
        pl.semaphore_signal(barrier, inc=1, device_id={"fsdp": lax.rem(me + k, n)}, device_id_type=pl.DeviceIdType.MESH)
    for k in range(1, teams):
        pl.semaphore_signal(barrier, inc=1, device_id={"ep": lax.rem(team + k, teams)}, device_id_type=pl.DeviceIdType.MESH)
    largest(0, 0)
    for t in range(2):
        for copy in measure_loads(1, t):
            copy.start()
    for t in range(2):
        for copy in send_loads(0, t):
            copy.start()
    pl.semaphore_wait(barrier, n + teams - 2)
    for t in range(2):
        if t:
            largest(0, t)
        for k in range(1, line):
            remote(own.at[0, t], zero.at[t, k - 1], y_send.at[t], y_recv.at[t], lax.rem(me + 2 * k, n)).start()
    measure(1)
    for t in range(2):
        wait_bytes(zero.at[t], y_send.at[t])
        wait_bytes(zero.at[t], y_recv.at[t])
        top = own[0, t]
        for k in range(1, line):
            top = jnp.maximum(top, zero[t, k - 1])
        mine[t] = top
        remote(mine.at[t], theirs.at[t], q_send.at[t], q_recv.at[t], partner).start()
    chip_max(1)
    spread(1)

    def early_max(e, carry):
        measure(e)
        chip_max(e)
        spread(e)
        return carry

    def step(i, carry):
        send(i, 0)

        @pl.when(i == 0)
        def _():
            lax.fori_loop(2, early, early_max, 0)

        stages(i, 0)
        send(i, 1)

        stages(i, 1)
        pl.when(i == 1)(router_cross)
        pl.when(i == experts // 4)(router_rows)
        pl.when(i == experts // 2)(router_columns)
        pl.when(i == experts - 2)(router_whole)
        return carry

    lax.fori_loop(0, experts, step, 0)
    for t, out in enumerate((sg, su)):
        for d in range(n):

            @pl.when(me == d)
            def _():
                out[...] = tops[t, :, d * width : (d + 1) * width]

    for slot in range(2):
        for t in range(2):
            wait_bytes(blocks.at[slot, t, pl.ds(0, n - 1)], send_sem.at[slot, t])
            wait_bytes(blocks.at[slot, t, 0], keep_sem.at[slot, t])

    def arrive(e, carry):
        for t in range(2):
            wait_bytes(outs[t].at[e, :, pl.ds(0, (n - 1) * rows)], recv_sem.at[t, e])
        return carry

    lax.fori_loop(0, experts, arrive, 0)


def settle(*refs):
    count = len(refs) // 2
    copies = []
    for src, dst in zip(refs[:count], refs[count:-1]):
        rows = src.shape[0]
        piece = max(rows // PIECES, 1) if len(src.shape) == 3 else rows
        for i in range(0, rows, piece):
            size = min(piece, rows - i)
            copies.append((src.at[pl.ds(i, size)], dst.at[pl.ds(i, size)]))
    copies = [pltpu.make_async_copy(src, dst, refs[-1].at[i]) for i, (src, dst) in enumerate(copies)]
    for copy in copies:
        copy.start()
    for copy in copies:
        copy.wait()


def per_device(n, teams, train_gate, other_gate, train_up, other_up, router_weight, router_gain):
    experts, rows, columns = train_gate.shape
    width = columns // n
    f32, bf16, dma = jnp.float32, jnp.bfloat16, pltpu.SemaphoreType.DMA
    ready = jax.ShapeDtypeStruct((experts, width, rows * n), bf16)
    any_space = pl.BlockSpec(memory_space=pl.ANY)
    part = router_weight.shape[::-1]
    scale = jax.ShapeDtypeStruct((experts, width), f32)
    out_shape = (ready, ready, scale, scale, jax.ShapeDtypeStruct((teams * part[0], n * part[1]), bf16))
    vmem = pl.BlockSpec(memory_space=pltpu.VMEM)
    outs = pl.pallas_call(
        functools.partial(regroup, n, teams),
        out_shape=out_shape,
        in_specs=[any_space] * 4 + [vmem],
        out_specs=(any_space, any_space, vmem, vmem, vmem),
        scratch_shapes=[
            pltpu.VMEM((2, 2, rows, columns), f32),
            pltpu.VMEM((2, 2, rows, columns), bf16),
            pltpu.VMEM((2, rows, columns), f32),
            pltpu.VMEM((2, rows, columns), bf16),
            pltpu.VMEM((columns, rows), f32),
            pltpu.VMEM((2, 2, n, width, rows), bf16),
            pltpu.VMEM((experts, 2, 1, columns), f32),
            *[pltpu.VMEM((experts, 1, columns), f32)] * 6,
            pltpu.VMEM((experts, n // 2 - 1, 1, columns), f32),
            pltpu.VMEM((2, n // 2 - 1, 1, columns), f32),
            pltpu.VMEM((2, 1, columns), f32),
            pltpu.VMEM((2, 1, columns), f32),
            pltpu.VMEM((experts, 2, 1, columns), f32),
            pltpu.VMEM((2, experts, columns), f32),
            pltpu.VMEM((n,) + part, bf16),
            pltpu.VMEM((teams, n) + part, bf16),
            dma((2, 2)),
            dma((2, 2)),
            dma((2,)),
            dma((2,)),
            dma((2, 2)),
            dma((2, 2)),
            dma((2, experts)),
            *[dma((experts,))] * 10,
            *[dma((2,))] * 4,
            *[dma] * 6,
        ],
        compiler_params=pltpu.CompilerParams(collective_id=0, has_side_effects=True, vmem_limit_bytes=28 * 2**20),
        name="regroup",
    )(train_gate, other_gate, train_up, other_up, (router_weight * router_gain[:, None]).astype(bf16).T)
    ready_gate, ready_up, scale_gate, scale_up, router = pl.pallas_call(
        settle,
        out_shape=out_shape,
        in_specs=[any_space] * 5,
        out_specs=(any_space,) * 5,
        scratch_shapes=[dma((2 * experts + 3,))],
        compiler_params=pltpu.CompilerParams(vmem_limit_bytes=2**20),
        name="settle",
    )(*outs)
    return jnp.swapaxes(ready_gate, 1, 2), jnp.swapaxes(ready_up, 1, 2), scale_gate, scale_up, router.T


def solution(mesh):
    in_specs = (
        P("ep", "fsdp", None),
        P("ep", "fsdp", None),
        P("ep", "fsdp", None),
        P("ep", "fsdp", None),
        P("fsdp", "ep"),
        P("fsdp"),
    )
    out_specs = (
        P("ep", None, "fsdp"),
        P("ep", None, "fsdp"),
        P("ep", "fsdp"),
        P("ep", "fsdp"),
        P(),
    )
    return jax.shard_map(
        functools.partial(per_device, mesh.shape["fsdp"], mesh.shape["ep"]), mesh=mesh, in_specs=in_specs, out_specs=out_specs,
        check_vma=False,
    )
```

time: 529 us -> 521 us (0.985)
  Pallas kernels: 527 us -> 519 us
    pallas_call x1, Pallas kernels: 519 us -> 511 us  [per_device(): pl.pallas_call(functools.partial(regroup, n, teams), out_shape=out_shape,...]
where the time goes in v2:
time: 521 us
  Pallas kernels  519 us (100%)
    pallas_call x1, Pallas kernels, per_device(): pl.pallas_call(functools.partial(regroup, n, teams), out_shape=out_shape,...  511 us

profile of v2, /device:TPU:0, one launch (start us, length us, event | category | flops | bytes accessed | tf_op | source)
XLA Modules:
  0.0 520.7 jit_solution(9085279880639751203)
XLA Ops:
  0.6 0.7 fusion.part
  1.4 511.2 %regroup.1 = (bf16[16,176,2048]{2,1,0:T(8,128)(2,1)S(1)}, bf16[16,176,2048]{2,1,0:T(8,128)(2,1)S(1)}, f32[16,176]{1,0:T(8,128)S(1)}, f32[16,176]{1,0:T(8,128)S(1)}, bf16[64,2048]{1,0:T(8,128)(2,1)S(1)}) custom-call(f32[16,256,1408]{2,1,0:T(8,128)} %tg.1, bf16[16,256,1408]{2,1,0:T(8,128)(2,1)} %og.1, f32[16,256,1408]{2,1,0:T(8,128)} %tu.1, ...), custom_call_target="tpu_custom_call" | custom-call | tf_op jit(solution)/shard_map/regroup/pallas_call | solution.py:332
  512.6 8.1 %settle.1 = (bf16[16,176,2048]{2,1,0:T(8,128)(2,1)}, bf16[16,176,2048]{2,1,0:T(8,128)(2,1)}, f32[16,176]{1,0:T(8,128)}, f32[16,176]{1,0:T(8,128)}, bf16[64,2048]{1,0:T(8,128)(2,1)}) custom-call(bf16[16,176,2048]{2,1,0:T(8,128)(2,1)S(1)} %get-tuple-element.15.refs_0_, bf16[16,176,2048]{2,1,0:T(8,128)(2,1)S(1)} %get-tuple-element.16.refs_1_, ...), custom_call_target="tpu_custom_call" | custom-call | tf_op jit(solution)/shard_map/settle/pallas_call | solution.py:368

commit v3 on v2

--- a/solution.py
+++ b/solution.py
@@ -9,13 +9,15 @@
 
 LANES = 128
 LAG = 1
+HEAD = 32
 PIECES = 8
 
 
-def regroup(n, teams, tg, og, tu, ou, part, rg, ru, sg, su, router, mx, mo, nx, no, turned, blocks,
-            own, pair, both, toright, toleft, fromleft, fromright, chips, zero, mine, theirs, final, tops, row, whole,
+def regroup(n, teams, tg, og, tu, ou, weight, gain, rg, ru, sg, su, router, mx, mo, nx, no, turned, blocks,
+            own, pair, both, toright, toleft, fromleft, fromright, chips, zero, mine, theirs, final, tops, held, gains, part, row, whole, lift, heads, tall, crown,
             mx_sem, mo_sem, nx_sem, no_sem, send_sem, keep_sem, recv_sem, p_send, p_recv, z_send, z_recv, r_send, r_recv,
-            l_send, l_recv, f_send, f_recv, y_send, y_recv, q_send, q_recv, a_send, a_recv, c_send, c_recv, b_send, b_recv):
+            l_send, l_recv, f_send, f_recv, y_send, y_recv, q_send, q_recv, a_send, a_recv, c_send, c_recv, b_send, b_recv, g_sem,
+            d_send, d_recv, d_keep):
     me, team = lax.axis_index("fsdp"), lax.axis_index("ep")
     core, chip = lax.rem(me, 2), lax.div(me, 2)
     partner = me + 1 - 2 * core
@@ -31,6 +33,8 @@
     trains, others, outs = (tg, tu), (og, ou), (rg, ru)
     ahead = [1 + (last - h) * LAG for h in range(line)]
     early = (ahead[0] + 1) // 2
+    head = heads.shape[1]
+    rest = pl.ds(head, width - head)
 
     def measure_loads(e, t):
         slot = lax.rem(e, 2)
@@ -61,6 +65,39 @@
         for j in range(0, columns, LANES):
             latest = mx[slot, t, :, j : j + LANES] + mo[slot, t, :, j : j + LANES].astype(jnp.float32)
             own[e, t, :, j : j + LANES] = jnp.max(jnp.abs(latest), axis=0, keepdims=True)
+
+    def zero_send(t):
+        for k in range(1, line):
+            remote(own.at[0, t], zero.at[t, k - 1], y_send.at[t], y_recv.at[t], lax.rem(me + 2 * k, n)).start()
+
+    def zero_max(t):
+        wait_bytes(zero.at[t], y_send.at[t])
+        wait_bytes(zero.at[t], y_recv.at[t])
+        top = own[0, t]
+        for k in range(1, line):
+            top = jnp.maximum(top, zero[t, k - 1])
+        mine[t] = top
+        remote(mine.at[t], theirs.at[t], q_send.at[t], q_recv.at[t], partner).start()
+
+    def head_turn(p):
+        j = pl.multiple_of(lax.rem(p + shift, count) * LANES, LANES)
+        latest = mx[0, 0, :, pl.ds(j, LANES)] + mo[0, 0, :, pl.ds(j, LANES)].astype(jnp.float32)
+        lift[pl.ds(j, LANES), :] = latest.T
+
+    def head_send(base, first):
+        for k in range(first, half):
+            d = base + lax.rem(me + k, half)
+            remote(lift.at[pl.ds(pl.multiple_of(d * width, width), head)], heads.at[me], d_send, d_recv, d).start()
+
+    def head_settle():
+        wait_bytes(heads.at[pl.ds(0, n - 1)], d_send)
+        wait_bytes(heads.at[pl.ds(0, n - 1)], d_recv)
+        for j in range(0, columns, LANES):
+            tall[j : j + LANES, :] = jnp.broadcast_to(final[0, 0, :, j : j + LANES], (LANES, LANES)).T
+        scale = tall[pl.ds(pl.multiple_of(me * width, width), head), 0:1]
+        for d in range(n):
+            crown[:, d * rows : (d + 1) * rows] = (heads[d] / scale).astype(jnp.bfloat16)
+        pltpu.make_async_copy(crown, rg.at[0, pl.ds(0, head)], d_keep).start()
 
     def measure(e):
         @pl.when(e + 1 < experts)
@@ -172,29 +209,44 @@
             latest = nx[t, :, pl.ds(j, LANES)] + no[t, :, pl.ds(j, LANES)].astype(jnp.float32)
             turned[pl.ds(j, LANES), :] = (latest / final[e, t, :, pl.ds(j, LANES)]).T
 
-        def pack(base, k):
+        def pack(base, k, here=False):
             d = base + lax.rem(me + k, half)
             blocks[slot, t, d] = turned[pl.ds(pl.multiple_of(d * width, width), width), :].astype(jnp.bfloat16)
-            if k == 0:
-                pl.when(d == me)(lambda: pltpu.make_async_copy(blocks.at[slot, t, d], place, keep_sem.at[slot, t]).start())
-                pl.when(d != me)(lambda: remote(blocks.at[slot, t, d], place, send_sem.at[slot, t], recv_sem.at[t, e], d).start())
+            block = blocks.at[slot, t, d]
+
+            def go(src, dst):
+                if here:
+                    pltpu.make_async_copy(src, dst, keep_sem.at[slot, t]).start()
+                else:
+                    remote(src, dst, send_sem.at[slot, t], recv_sem.at[t, e], d).start()
+
+            if t == 0:
+                pl.when(e == 0)(lambda: go(block.at[rest], place.at[rest]))
+                pl.when(e > 0)(lambda: go(block, place))
             else:
-                remote(blocks.at[slot, t, d], place, send_sem.at[slot, t], recv_sem.at[t, e], d).start()
+                go(block, place)
 
         for p in range(count - skipped):
             turn(p)
 
-        @pl.when(e >= 2)
+        @pl.when(e >= (2 if t else 3))
         def _():
             wait_bytes(blocks.at[slot, t, pl.ds(0, n - 1)], send_sem.at[slot, t])
             wait_bytes(blocks.at[slot, t, 0], keep_sem.at[slot, t])
+
+        if t == 0:
+
+            @pl.when(e == 2)
+            def _():
+                wait_bytes(blocks.at[0, 0, pl.ds(0, n - 1), rest], send_sem.at[0, 0])
+                wait_bytes(blocks.at[0, 0, 0, rest], keep_sem.at[0, 0])
 
         for k in range(half):
             pack(far, k)
         for p in range(count - skipped, count):
             turn(p)
         for k in range(half):
-            pack(near, k)
+            pack(near, k, k == 0)
 
         @pl.when(e + 1 < experts)
         def _():
@@ -202,6 +254,9 @@
                 copy.start()
 
     def router_cross():
+        for copy in router_loads:
+            copy.wait()
+        part[...] = (held[...] * gains[...]).astype(jnp.bfloat16)
         row[me] = part[...]
         remote(part, row.at[me], a_send, a_recv, mirror).start()
 
@@ -226,38 +281,33 @@
             for d in range(n):
                 router[a * wide : (a + 1) * wide, d * deep : (d + 1) * deep] = whole[a, d]
 
-    for t in range(2):
-        for copy in measure_loads(0, t):
-            copy.start()
+    for copy in measure_loads(0, 0):
+        copy.start()
     barrier = pltpu.get_barrier_semaphore()
     for k in range(1, n):
         pl.semaphore_signal(barrier, inc=1, device_id={"fsdp": lax.rem(me + k, n)}, device_id_type=pl.DeviceIdType.MESH)
     for k in range(1, teams):
         pl.semaphore_signal(barrier, inc=1, device_id={"ep": lax.rem(team + k, teams)}, device_id_type=pl.DeviceIdType.MESH)
+    router_loads = (pltpu.make_async_copy(weight, held, g_sem.at[0]), pltpu.make_async_copy(gain, gains, g_sem.at[1]))
+    loads = [*measure_loads(0, 1), *measure_loads(1, 0), *measure_loads(1, 1), *send_loads(0, 0), *send_loads(0, 1), *router_loads]
+    for copy in loads:
+        copy.start()
     largest(0, 0)
-    for t in range(2):
-        for copy in measure_loads(1, t):
-            copy.start()
-    for t in range(2):
-        for copy in send_loads(0, t):
-            copy.start()
+    for p in range(count - skipped):
+        head_turn(p)
     pl.semaphore_wait(barrier, n + teams - 2)
-    for t in range(2):
-        if t:
-            largest(0, t)
-        for k in range(1, line):
-            remote(own.at[0, t], zero.at[t, k - 1], y_send.at[t], y_recv.at[t], lax.rem(me + 2 * k, n)).start()
+    zero_send(0)
+    head_send(far, 0)
+    largest(0, 1)
+    zero_send(1)
+    for p in range(count - skipped, count):
+        head_turn(p)
+    head_send(near, 1)
+    heads[me] = lift[pl.ds(pl.multiple_of(me * width, width), head), :]
     measure(1)
-    for t in range(2):
-        wait_bytes(zero.at[t], y_send.at[t])
-        wait_bytes(zero.at[t], y_recv.at[t])
-        top = own[0, t]
-        for k in range(1, line):
-            top = jnp.maximum(top, zero[t, k - 1])
-        mine[t] = top
-        remote(mine.at[t], theirs.at[t], q_send.at[t], q_recv.at[t], partner).start()
     chip_max(1)
     spread(1)
+    zero_max(0)
 
     def early_max(e, carry):
         measure(e)
@@ -270,6 +320,7 @@
 
         @pl.when(i == 0)
         def _():
+            zero_max(1)
             lax.fori_loop(2, early, early_max, 0)
 
         stages(i, 0)
@@ -277,6 +328,7 @@
 
         stages(i, 1)
         pl.when(i == 1)(router_cross)
+        pl.when(i == 2)(head_settle)
         pl.when(i == experts // 4)(router_rows)
         pl.when(i == experts // 2)(router_columns)
         pl.when(i == experts - 2)(router_whole)
@@ -300,7 +352,10 @@
             wait_bytes(outs[t].at[e, :, pl.ds(0, (n - 1) * rows)], recv_sem.at[t, e])
         return carry
 
-    lax.fori_loop(0, experts, arrive, 0)
+    wait_bytes(rg.at[0, rest, pl.ds(0, (n - 1) * rows)], recv_sem.at[0, 0])
+    wait_bytes(ru.at[0, :, pl.ds(0, (n - 1) * rows)], recv_sem.at[1, 0])
+    lax.fori_loop(1, experts, arrive, 0)
+    pltpu.make_async_copy(crown, rg.at[0, pl.ds(0, head)], d_keep).wait()
 
 
 def settle(*refs):
@@ -325,14 +380,16 @@
     f32, bf16, dma = jnp.float32, jnp.bfloat16, pltpu.SemaphoreType.DMA
     ready = jax.ShapeDtypeStruct((experts, width, rows * n), bf16)
     any_space = pl.BlockSpec(memory_space=pl.ANY)
+    head = min(HEAD, width // 2)
     part = router_weight.shape[::-1]
+    in_hbm = functools.partial(pltpu.with_memory_space_constraint, memory_space=pltpu.HBM)
     scale = jax.ShapeDtypeStruct((experts, width), f32)
     out_shape = (ready, ready, scale, scale, jax.ShapeDtypeStruct((teams * part[0], n * part[1]), bf16))
     vmem = pl.BlockSpec(memory_space=pltpu.VMEM)
     outs = pl.pallas_call(
         functools.partial(regroup, n, teams),
         out_shape=out_shape,
-        in_specs=[any_space] * 4 + [vmem],
+        in_specs=[any_space] * 6,
         out_specs=(any_space, any_space, vmem, vmem, vmem),
         scratch_shapes=[
             pltpu.VMEM((2, 2, rows, columns), f32),
@@ -349,8 +406,15 @@
             pltpu.VMEM((2, 1, columns), f32),
             pltpu.VMEM((experts, 2, 1, columns), f32),
             pltpu.VMEM((2, experts, columns), f32),
+            pltpu.VMEM(part, f32),
+            pltpu.VMEM((1, part[1]), f32),
+            pltpu.VMEM(part, bf16),
             pltpu.VMEM((n,) + part, bf16),
             pltpu.VMEM((teams, n) + part, bf16),
+            pltpu.VMEM((columns, rows), f32),
+            pltpu.VMEM((n, head, rows), f32),
+            pltpu.VMEM((columns, LANES), f32),
+            pltpu.VMEM((head, rows * n), bf16),
             dma((2, 2)),
             dma((2, 2)),
             dma((2,)),
@@ -361,10 +425,12 @@
             *[dma((experts,))] * 10,
             *[dma((2,))] * 4,
             *[dma] * 6,
+            dma((2,)),
+            *[dma] * 3,
         ],
         compiler_params=pltpu.CompilerParams(collective_id=0, has_side_effects=True, vmem_limit_bytes=28 * 2**20),
         name="regroup",
-    )(train_gate, other_gate, train_up, other_up, (router_weight * router_gain[:, None]).astype(bf16).T)
+    )(train_gate, other_gate, train_up, other_up, in_hbm(router_weight.T), in_hbm(router_gain[None]))
     ready_gate, ready_up, scale_gate, scale_up, router = pl.pallas_call(
         settle,
         out_shape=out_shape,

time: 521 us -> 518 us (level)
  no operation moved by 1% of the time
where the time goes in v3:
time: 518 us
  Pallas kernels  518 us (100%)
    pallas_call x1, Pallas kernels, per_device(): pl.pallas_call(functools.partial(regroup, n, teams), out_shape=out_shape,...  509 us

profile of v3, /device:TPU:0, one launch (start us, length us, event | category | flops | bytes accessed | tf_op | source)
XLA Modules:
  0.0 518.2 jit_solution(6497611696951074641)
XLA Ops:
  0.6 509.4 %regroup.1 = (bf16[16,176,2048]{2,1,0:T(8,128)(2,1)S(1)}, bf16[16,176,2048]{2,1,0:T(8,128)(2,1)S(1)}, f32[16,176]{1,0:T(8,128)S(1)}, f32[16,176]{1,0:T(8,128)S(1)}, bf16[64,2048]{1,0:T(8,128)(2,1)S(1)}) custom-call(f32[16,256,1408]{2,1,0:T(8,128)} %tg.1, bf16[16,256,1408]{2,1,0:T(8,128)(2,1)} %og.1, f32[16,256,1408]{2,1,0:T(8,128)} %tu.1, ...), custom_call_target="tpu_custom_call" | custom-call | tf_op jit(solution)/shard_map/regroup/pallas_call | solution.py:389
  510.1 8.1 %settle.1 = (bf16[16,176,2048]{2,1,0:T(8,128)(2,1)}, bf16[16,176,2048]{2,1,0:T(8,128)(2,1)}, f32[16,176]{1,0:T(8,128)}, f32[16,176]{1,0:T(8,128)}, bf16[64,2048]{1,0:T(8,128)(2,1)}) custom-call(bf16[16,176,2048]{2,1,0:T(8,128)(2,1)S(1)} %get-tuple-element.15.refs_0_, bf16[16,176,2048]{2,1,0:T(8,128)(2,1)S(1)} %get-tuple-element.16.refs_1_, ...), custom_call_target="tpu_custom_call" | custom-call | tf_op jit(solution)/shard_map/settle/pallas_call | solution.py:434
